TPU v7x, 128 devices: a whole 4x4x4 slice. The times are simulated.
128 devices in a mesh: dp: 1, tp: 2 (over core), ep: 64 (over z, y, x).
Axes of the slice: x: 4, y: 4, z: 4, core: 2. Of those that a mesh axis runs over, the one named last changes fastest.
Arguments:
- x: bfloat16 [64, 1024, 768], P(('dp', 'ep'))
- src_len: int32 [64], P(('dp', 'ep'))
- expert_idx: int32 [64, 1024, 2], P(('dp', 'ep'))
- ln_gain: float32 [4, 768], replicated
- ln_bias: float32 [4, 768], replicated
- w_query: bfloat16 [2, 768, 12, 64], P(None, None, 'tp')
- b_query: float32 [2, 12, 64], P(None, 'tp')
- w_key: bfloat16 [2, 768, 12, 64], P(None, None, 'tp')
- w_value: bfloat16 [2, 768, 12, 64], P(None, None, 'tp')
- b_value: float32 [2, 12, 64], P(None, 'tp')
- w_attn_out: bfloat16 [2, 12, 64, 768], P(None, 'tp')
- b_attn_out: float32 [2, 768], replicated
- w_fc1: bfloat16 [768, 3072], P(None, 'tp')
- b_fc1: float32 [3072], P('tp')
- w_fc2: bfloat16 [3072, 768], P('tp')
- b_fc2: float32 [768], replicated
- w_router: float32 [768, 128], replicated
- w_exp_in: bfloat16 [128, 768, 3072], P('ep', None, 'tp')
- b_exp_in: float32 [128, 3072], P('ep', 'tp')
- w_exp_out: bfloat16 [128, 3072, 768], P('ep', 'tp')
- b_exp_out: float32 [128, 768], P('ep')
Outputs:
- output: bfloat16 [64, 1024, 768], P(('dp', 'ep'))
All inputs are finite; a program needn't handle non-finite values.
Results may differ from a plain program's by a relative error of at most 0.0133347.
Values are sent between devices in bfloat16 or wider.
A program may use at most 1 GiB of HBM per device.

v0:
```python
import functools

import jax
import jax.numpy as jnp
from jax import lax
from jax.experimental import pallas as pl
from jax.experimental.pallas import tpu as pltpu
from jax.sharding import PartitionSpec as P

LN_EPS = 1e-5
MESH = pl.DeviceIdType.MESH
F32 = jnp.float32
BF16 = jnp.bfloat16
MIN_LEN = 256


def dot_nn(a, b):
    return lax.dot_general(a, b, (((1,), (0,)), ((), ())), preferred_element_type=F32)


def dot_nt(a, b):
    return lax.dot_general(a, b, (((1,), (1,)), ((), ())), preferred_element_type=F32)


def layer_norm(block, gain, shift):
    block = block.astype(F32)
    centered = block - jnp.mean(block, axis=-1, keepdims=True)
    variance = jnp.mean(centered * centered, axis=-1, keepdims=True)
    return centered * lax.rsqrt(variance + LN_EPS) * gain + shift


def iota(shape, axis):
    return lax.broadcasted_iota(jnp.int32, shape, axis)


def offset_peers(ep_size, me, step):
    if ep_size != 64:
        return lax.rem(me + step, ep_size), lax.rem(me + ep_size - step, ep_size)
    dy, dx = lax.rem(step // 4, 4), lax.rem(step, 4)
    dz = lax.rem(step // 16 + 8 - dy - dx, 4)
    z, y, x = me // 16, lax.rem(me // 4, 4), lax.rem(me, 4)
    ahead = lax.rem(z + dz, 4) * 16 + lax.rem(y + dy, 4) * 4 + lax.rem(x + dx, 4)
    behind = lax.rem(z + 4 - dz, 4) * 16 + lax.rem(y + 4 - dy, 4) * 4 + lax.rem(x + 4 - dx, 4)
    return ahead, behind


def offset_step(ep_size, me, device):
    if ep_size != 64:
        delta = device - me
        return jnp.where(delta < 0, delta + ep_size, delta)
    z, y, x = me // 16, lax.rem(me // 4, 4), lax.rem(me, 4)
    dz, dy, dx = ((device >> 4) - z) & 3, (((device >> 2) & 3) - y) & 3, ((device & 3) - x) & 3
    return (((dz + dy + dx) & 3) << 4) + (dy << 2) + dx


def encoder_kernel(ep_size, groups, block, chunk, len_ref, idx_ref, x_hbm, gain_ref, shift_ref, wq_hbm, wk_hbm, wv_hbm, wo_hbm, bq_ref, bv_ref, bo_ref, f1_hbm, fb1_ref, f2_hbm, fb2_ref, wr_hbm, e1_hbm, eb1_ref, e2_hbm, eb2_ref, out_ref,
                   hid_ref, wq_ref, wk_ref, wv_ref, wo_ref, f1_ref, f2_ref, wr_ref, e1_ref, e2_ref, load_sem, x_sem,
                   q_ref, kx_ref, vx_ref, ctx_ref, s_even, s_odd, p_even, p_odd, head_ref, part_ref, recv_ref, part_send, part_recv,
                   norm_ref, logit_ref, dest_ref, meta_ref, disp_ref, mine_ref, other_ref, keep_ref, give_ref, take_ref, done_ref, ret_ref,
                   ship_send, ship_recv, swap_send, swap_recv, give_send, give_recv, back_send, back_recv, acc_ref, near_ref, far_ref, half_send, half_recv):
    me, core = lax.axis_index('ep'), lax.axis_index('tp')
    tokens, d_model = hid_ref.shape
    steps = tokens // block
    width = q_ref.shape[1]
    local_experts, cap, half = disp_ref.shape[2:]
    experts = wr_ref.shape[1]
    each = ep_size // groups
    near = pl.ds(pl.multiple_of(core * half, half), half)
    far = pl.ds(pl.multiple_of((1 - core) * half, half), half)
    barrier = pltpu.get_barrier_semaphore()

    def rows_of(step):
        return pl.ds(pl.multiple_of(step * block, block), block)

    def to_partner(src, dst, send_sem, recv_sem):
        return pltpu.make_async_remote_copy(src_ref=src, dst_ref=dst, send_sem=send_sem, recv_sem=recv_sem, device_id={'tp': 1 - core}, device_id_type=MESH)

    def x_copy(step):
        return pltpu.make_async_copy(x_hbm.at[rows_of(step)], hid_ref.at[rows_of(step)], x_sem.at[step])

    pairs = [(wq_hbm, wq_ref), (wk_hbm, wk_ref), (wv_hbm, wv_ref), (wo_hbm, wo_ref), (f1_hbm, f1_ref), (f2_hbm, f2_ref), (wr_hbm, wr_ref), (e1_hbm, e1_ref), (e2_hbm, e2_ref)]
    loads = [pltpu.make_async_copy(src, dst, load_sem.at[index]) for index, (src, dst) in enumerate(pairs)]
    load_q, load_k, load_v, load_o, load_f1, load_f2, load_r, load_e1, load_e2 = loads

    def fetch_x(step, carry):
        x_copy(step).start()
        return carry

    lax.fori_loop(0, steps, fetch_x, 0)
    for load in loads:
        load.start()

    def greet(step, carry):
        pl.semaphore_signal(barrier, inc=1, device_id={'ep': offset_peers(ep_size, me, step)[0]}, device_id_type=MESH)
        return carry

    lax.fori_loop(1, ep_size, greet, 0)
    pl.semaphore_signal(barrier, inc=1, device_id={'tp': 1 - core}, device_id_type=MESH)

    def exchange(stage, step):
        return to_partner(part_ref.at[rows_of(step)], recv_ref.at[stage % 2, rows_of(step)], part_send.at[stage, step], part_recv.at[stage, step])

    def absorb(stage, step, bias):
        exchange(stage, step).wait()
        total = part_ref[rows_of(step)].astype(F32) + recv_ref[stage % 2, rows_of(step)].astype(F32)
        hidden = (hid_ref[rows_of(step)].astype(F32) + total + bias).astype(BF16)
        hid_ref[rows_of(step)] = hidden
        return hidden

    lane = iota((block, 128), 1)
    key_ok = iota((chunk, tokens - MIN_LEN), 1) + MIN_LEN < len_ref[0] if tokens > MIN_LEN else None

    def softmax(s_ref, p_ref):
        for start in range(0, block, chunk):
            scores = s_ref[start:start + chunk]
            if key_ok is not None:
                scores = jnp.concatenate([scores[:, :MIN_LEN], jnp.where(key_ok, scores[:, MIN_LEN:], -1e30)], axis=1)
            weights = jnp.exp(scores - jnp.max(scores, axis=-1, keepdims=True))
            scale = 1.0 / jnp.sum(weights, axis=-1, keepdims=True)
            p_ref[start:start + chunk] = (weights * scale).astype(BF16)

    def project(layer, step, normed):
        rows = rows_of(step)
        bias_q, bias_v = bq_ref[layer], bv_ref[layer]
        query = (dot_nt(normed, wq_ref[layer]) + bias_q).astype(BF16)
        q_ref[rows] = (query.astype(F32) * 0.125).astype(BF16)
        keys = dot_nt(normed, wk_ref[layer])
        values = dot_nt(normed, wv_ref[layer]) + bias_v
        for head in range(width // 64):
            lanes = slice(128 * (head // 2), 128 * (head // 2) + 128)
            mine = (lane < 64) if head % 2 == 0 else (lane >= 64)
            kx_ref[head, rows] = jnp.where(mine, keys[:, lanes], 0.0).astype(BF16)
            vx_ref[head, rows] = jnp.where(mine, values[:, lanes], 0.0).astype(BF16)

    def attend(layer, stage):
        heads = width // 64
        s_refs, p_refs = (s_even, s_odd), (p_even, p_odd)

        def score(rows, head):
            lanes = slice(128 * (head // 2), 128 * (head // 2) + 128)
            s_refs[head % 2][...] = dot_nt(q_ref[rows, lanes], kx_ref[head])

        def weigh(head):
            lanes = slice(128 * (head // 2), 128 * (head // 2) + 128)
            mixed = dot_nn(p_refs[head % 2][...], vx_ref[head])
            if head % 2 == 0:
                head_ref[...] = mixed
            else:
                ctx_ref[:, lanes] = (head_ref[...] + mixed).astype(BF16)

        def body(step, carry):
            rows = rows_of(step)
            score(rows, 0)
            for head in range(heads + 1):
                if head + 1 < heads:
                    score(rows, head + 1)
                if head > 0:
                    weigh(head - 1)
                if head < heads:
                    softmax(s_refs[head % 2], p_refs[head % 2])
            part_ref[rows] = dot_nn(ctx_ref[...], wo_ref[layer]).astype(BF16)
            exchange(stage, step).start()
            return carry

        lax.fori_loop(0, steps, body, 0)

    def normed_hidden(hidden, norm):
        return layer_norm(hidden, gain_ref[norm:norm + 1], shift_ref[norm:norm + 1]).astype(BF16)

    load_q.wait()
    load_k.wait()
    load_v.wait()

    def first_project(step, carry):
        x_copy(step).wait()
        project(0, step, normed_hidden(hid_ref[rows_of(step)], 0))
        return carry

    lax.fori_loop(0, steps, first_project, 0)
    load_o.wait()
    pl.semaphore_wait(barrier, ep_size)
    attend(0, 0)
    load_f1.wait()
    load_f2.wait()

    def feed(step, carry):
        normed = normed_hidden(absorb(0, step, bo_ref[0:1]), 1)
        inner = jnp.maximum(dot_nn(normed, f1_ref[...]) + fb1_ref[...], 0.0).astype(BF16)
        part_ref[rows_of(step)] = dot_nn(inner, f2_ref[...]).astype(BF16)
        exchange(1, step).start()
        return carry

    lax.fori_loop(0, steps, feed, 0)

    def second_project(step, carry):
        project(1, step, normed_hidden(absorb(1, step, fb2_ref[...]), 2))
        return carry

    lax.fori_loop(0, steps, second_project, 0)
    attend(1, 2)

    valid = iota((1, tokens), 1) < len_ref[0]
    first, second = idx_ref[0:1], idx_ref[1:2]
    expert = iota((experts, tokens), 0)
    hot_first = jnp.where((expert == first) & valid, 1.0, 0.0)
    hot_second = jnp.where((expert == second) & valid, 1.0, 0.0)
    earlier = jnp.where(iota((tokens, tokens), 0) < iota((tokens, tokens), 1), 1.0, 0.0).astype(BF16)
    rank_first = dot_nn(hot_first.astype(BF16), earlier)
    rank_second = dot_nn(hot_second.astype(BF16), earlier) + jnp.sum(hot_first, axis=1, keepdims=True)
    slot_first = jnp.sum(rank_first * hot_first, axis=0, keepdims=True).astype(jnp.int32)
    slot_second = jnp.sum(rank_second * hot_second, axis=0, keepdims=True).astype(jnp.int32)

    def place(choice, slot):
        step = offset_step(ep_size, me, choice >> 1)
        return jnp.where(valid & (slot < cap), ((step << 1) + (choice & 1)) * cap + slot, experts * cap)

    dest_ref[0:1] = place(first, slot_first)
    dest_ref[1:2] = place(second, slot_second)
    load_r.wait()
    router = wr_ref[...].astype(BF16)

    def settle(step, carry):
        normed = normed_hidden(absorb(2, step, bo_ref[1:2]), 3)
        norm_ref[rows_of(step)] = normed
        logit_ref[rows_of(step)] = dot_nn(normed, router)
        return carry

    lax.fori_loop(0, steps, settle, 0)

    def slot_rows(step):
        return pl.ds(pl.multiple_of(lax.rem(step, each) * cap, cap), cap)

    def ship(step):
        ahead, _ = offset_peers(ep_size, me, step)
        return pltpu.make_async_remote_copy(src_ref=disp_ref.at[step // each, lax.rem(step, each)], dst_ref=mine_ref.at[step // each, :, slot_rows(step)], send_sem=ship_send.at[step], recv_sem=ship_recv.at[step], device_id={'ep': ahead}, device_id_type=MESH)

    def ship_back(step):
        _, behind = offset_peers(ep_size, me, step)
        return pltpu.make_async_remote_copy(src_ref=done_ref.at[step // each, :, slot_rows(step)], dst_ref=ret_ref.at[step // each, lax.rem(step, each)], send_sem=back_send.at[step], recv_sem=back_recv.at[step], device_id={'ep': behind}, device_id_type=MESH)

    def swap(group):
        return to_partner(mine_ref.at[group], other_ref.at[group], swap_send.at[group], swap_recv.at[group])

    def give(group):
        return to_partner(give_ref.at[group], take_ref.at[group], give_send.at[group], give_recv.at[group])

    def each_step(group, act):
        def body(step, carry):
            act(step)
            return carry

        lax.fori_loop(jnp.where(group == 0, 1, group * each), (group + 1) * each, body, 0)

    members = each * local_experts * cap

    def scatter(group, carry):
        slots = iota((members, tokens), 0) + group * members
        taken = jnp.where((slots == dest_ref[0:1]) | (slots == dest_ref[1:2]), 1.0, 0.0).astype(BF16)
        disp_ref[group] = dot_nn(taken, norm_ref[:, near]).astype(BF16).reshape(each, local_experts, cap, half)
        each_step(group, lambda step: ship(step).start())
        return carry

    lax.fori_loop(0, groups, scatter, 0)
    mine_ref[0, :, 0:cap] = disp_ref[0, 0]

    row_id = iota((128, tokens), 0)
    packed = jnp.where(row_id == 0, dest_ref[0:1], jnp.where(row_id == 1, dest_ref[1:2], jnp.where(row_id == 2, first, second)))
    meta_ref[...] = packed.astype(F32).T
    column = iota((block, experts), 1).astype(F32)
    spot = iota((block, 128), 1)

    def gate(step, carry):
        table, logits = meta_ref[rows_of(step)], logit_ref[rows_of(step)]
        logit_first = jnp.sum(jnp.where(column == table[:, 2:3], logits, 0.0), axis=1, keepdims=True)
        logit_second = jnp.sum(jnp.where(column == table[:, 3:4], logits, 0.0), axis=1, keepdims=True)
        gate_first = jax.nn.sigmoid(logit_first - logit_second)
        gate_second = jax.nn.sigmoid(logit_second - logit_first)
        meta_ref[rows_of(step)] = jnp.where(spot == 2, gate_first, jnp.where(spot == 3, gate_second, table))
        acc_ref[rows_of(step)] = hid_ref[rows_of(step), near].astype(F32)
        return carry

    lax.fori_loop(0, steps, gate, 0)
    load_e1.wait()
    load_e2.wait()

    def deliver(group):
        give(group).wait_recv()
        for expert in range(local_experts):
            total = keep_ref[expert].astype(F32) + take_ref[group, expert].astype(F32)
            done_ref[group, expert] = (total + eb2_ref[expert:expert + 1, near]).astype(BF16)
        each_step(group, lambda step: ship_back(step).start())

    def work(group, carry):
        each_step(group, lambda step: ship(step).wait_recv())
        swap(group).start()

        @pl.when(group > 0)
        def _():
            deliver(group - 1)

        swap(group).wait_recv()
        for expert in range(local_experts):
            inner = dot_nn(mine_ref[group, expert], e1_ref[expert, near]) + dot_nn(other_ref[group, expert], e1_ref[expert, far])
            inner = jnp.maximum(inner + eb1_ref[expert:expert + 1], 0.0).astype(BF16)
            give_ref[group, expert] = dot_nn(inner, e2_ref[expert, :, far]).astype(BF16)
            keep_ref[expert] = dot_nn(inner, e2_ref[expert, :, near]).astype(BF16)
        give(group).start()
        return carry

    lax.fori_loop(0, groups, work, 0)
    deliver(groups - 1)
    ret_ref[0, 0] = done_ref[0, :, 0:cap]

    def halves(step):
        return to_partner(near_ref.at[rows_of(step)], far_ref.at[rows_of(step)], half_send.at[step], half_recv.at[step])

    def gather(group, carry):
        each_step(group, lambda step: ship_back(step).wait_recv())
        slots = iota((block, members), 1) + group * members

        def pick(step, carry):
            rows = rows_of(step)
            table = meta_ref[rows]
            dest = table.astype(jnp.int32)
            returned = ret_ref[group].reshape(members, half)
            one = dot_nn(jnp.where(slots == dest[:, 0:1], 1.0, 0.0).astype(BF16), returned)
            two = dot_nn(jnp.where(slots == dest[:, 1:2], 1.0, 0.0).astype(BF16), returned)
            result = acc_ref[rows] + (table[:, 2:3] * one + table[:, 3:4] * two)
            acc_ref[rows] = result

            @pl.when(group == groups - 1)
            def _():
                near_ref[rows] = result.astype(BF16)
                halves(step).start()
                out_ref[rows, near] = result.astype(BF16)

            return carry

        lax.fori_loop(0, steps, pick, 0)
        return carry

    lax.fori_loop(0, groups, gather, 0)

    def finish(step, carry):
        halves(step).wait()
        out_ref[rows_of(step), far] = far_ref[rows_of(step)]
        return carry

    lax.fori_loop(0, steps, finish, 0)

    def drain(step, carry):
        ship(step).wait_send()
        ship_back(step).wait_send()
        return carry

    lax.fori_loop(1, ep_size, drain, 0)

    def drain_pairs(group, carry):
        swap(group).wait_send()
        give(group).wait_send()
        return carry

    lax.fori_loop(0, groups, drain_pairs, 0)


def solution(mesh):
    ep_size = mesh.shape['ep']

    def local_fn(x, src_len, expert_idx, ln_gain, ln_bias, w_query, b_query, w_key, w_value, b_value, w_attn_out, b_attn_out, w_fc1, b_fc1, w_fc2, b_fc2, w_router, w_exp_in, b_exp_in, w_exp_out, b_exp_out):
        _, tokens, d_model = x.shape
        width = w_query.shape[2] * w_query.shape[3]
        num_experts = w_router.shape[1]
        local_experts, _, hidden = w_exp_in.shape
        cap = 2 * (-(-tokens // num_experts))
        half = d_model // 2
        groups = 4 if ep_size >= 16 else 2
        each = ep_size // groups
        block, chunk = min(256, tokens // 2), 32
        steps = tokens // block
        w_q, w_k, w_v = (jnp.transpose(w, (0, 2, 3, 1)).reshape(2, width, d_model) for w in (w_query, w_key, w_value))
        w_o = w_attn_out.reshape(2, width, d_model)
        idx = jnp.transpose(expert_idx, (0, 2, 1)).reshape(2, tokens)
        vmem = lambda *shape: pltpu.VMEM(shape, BF16)
        vmem32 = lambda *shape: pltpu.VMEM(shape, F32)
        dma = lambda *shape: pltpu.SemaphoreType.DMA(shape)
        whole = pl.BlockSpec(memory_space=pltpu.VMEM)
        far_away = pl.BlockSpec(memory_space=pl.ANY)
        rows = each * cap
        wide = vmem(groups, local_experts, rows, half)
        blocks = vmem(groups, each, local_experts, cap, half)
        result = pl.pallas_call(
            functools.partial(encoder_kernel, ep_size, groups, block, chunk),
            out_shape=jax.ShapeDtypeStruct((tokens, d_model), BF16),
            in_specs=[pl.BlockSpec(memory_space=pltpu.SMEM), whole, far_away, whole, whole, far_away, far_away, far_away, far_away, whole, whole, whole, far_away, whole, far_away, whole, far_away, far_away, whole, far_away, whole],
            out_specs=whole,
            scratch_shapes=[
                vmem(tokens, d_model), vmem(2, width, d_model), vmem(2, width, d_model), vmem(2, width, d_model), vmem(2, width, d_model), vmem(*w_fc1.shape), vmem(*w_fc2.shape), vmem32(*w_router.shape), vmem(*w_exp_in.shape), vmem(*w_exp_out.shape), dma(9), dma(steps),
                vmem(tokens, width), vmem(width // 64, tokens, 128), vmem(width // 64, tokens, 128), vmem(block, width), vmem32(block, tokens), vmem32(block, tokens), vmem(block, tokens), vmem(block, tokens), vmem32(block, 128), vmem(tokens, d_model), vmem(2, tokens, d_model), dma(3, steps), dma(3, steps),
                vmem(tokens, d_model), vmem32(tokens, num_experts), pltpu.VMEM((8, tokens), jnp.int32), vmem32(tokens, 128), blocks, wide, wide, vmem(local_experts, rows, half), wide, wide, wide, blocks,
                dma(ep_size), dma(ep_size), dma(groups), dma(groups), dma(groups), dma(groups), dma(ep_size), dma(ep_size), vmem32(tokens, half), vmem(tokens, half), vmem(tokens, half), dma(steps), dma(steps),
            ],
            compiler_params=pltpu.CompilerParams(collective_id=1, has_side_effects=True, vmem_limit_bytes=67043328),
        )(src_len, idx, x.reshape(tokens, d_model), ln_gain, ln_bias, w_q, w_k, w_v, w_o, b_query.reshape(2, 1, width), b_value.reshape(2, 1, width), b_attn_out, w_fc1, b_fc1.reshape(1, -1), w_fc2, b_fc2.reshape(1, -1), w_router, w_exp_in, b_exp_in, w_exp_out, b_exp_out)
        return result.reshape(1, tokens, d_model)

    in_specs = (P(('dp', 'ep'), None, None), P(('dp', 'ep')), P(('dp', 'ep'), None, None), P(), P(), P(None, None, 'tp', None), P(None, 'tp', None), P(None, None, 'tp', None), P(None, None, 'tp', None), P(None, 'tp', None), P(None, 'tp', None, None), P(), P(None, 'tp'), P('tp'), P('tp', None), P(), P(), P('ep', None, 'tp'), P('ep', 'tp'), P('ep', 'tp', None), P('ep', None))
    return jax.shard_map(local_fn, mesh=mesh, in_specs=in_specs, out_specs=P(('dp', 'ep'), None, None), check_vma=False)
```

profile of v0, /device:TPU:1, one launch (start us, length us, event | category | flops | bytes accessed | tf_op | source)
XLA Modules:
  0.0 116.1 jit_solution(2769548041422982281)
XLA Ops:
  0.7 1.3 %reshape.42.fb2_ref = f32[1,768]{1,0:T(1,128)} reshape(f32[768]{0:T(1024)} %param.36) | data formatting | bytes 6144 | tf_op jit(solution)/shard_map/reshape | solution.py:403
  1.9 1.3 %reshape.41.fb1_ref = f32[1,1536]{1,0:T(1,128)} reshape(f32[1536]{0:T(1024)} %param.34) | data formatting | bytes 12288 | tf_op jit(solution)/shard_map/reshape | solution.py:403
  3.2 0.7 copy.24
  3.9 0.7 reshape.44.bq_ref
  4.6 0.7 copy.25
  5.3 0.7 reshape.45.bv_ref
  5.9 107.5 %shard_map.199 = bf16[1024,768]{1,0:T(8,128)(2,1)} custom-call(s32[1]{0:T(128)S(6)} %copy.29.len_ref, s32[2,1024]{1,0:T(2,128)} %bitcast.21, bf16[1024,768]{1,0:T(8,128)(2,1)} %bitcast.16, f32[4,768]{1,0:T(4,128)} %gain_ref.1, f32[4,768]{1,0:T(4,128)} %shift_ref.1, bf16[2,384,768]{2,1,0:T(8,128)(2,1)} %bitcast.17, bf16[2,384,768]{2,1,0:T(8,128)(2,1)} %bitcast.18, ...), custom_call_target="tpu_custom_call" | custom-call | tf_op jit(solution)/shard_map/pallas_call | solution.py:391
  113.4 2.7 %copy.30 = bf16[1,1024,768]{2,1,0:T(8,128)(2,1)} copy(bf16[1,1024,768]{2,1,0:T(8,128)(2,1)} %bitcast.15) | data formatting | bytes 3145728
where the time goes:
time: 116 us
  Pallas kernels  108 us (93%)
  local copies, waits for them, and re-layouts  7.91 us (7%)
    pallas_call x1, Pallas kernels, local_fn(): pl.pallas_call(functools.partial(encoder_kernel, ep_size, groups, block,...  108 us
    unnamed x3, local copies, waits for them, and re-layouts  4.04 us

commit v1 on v0

--- a/solution.py
+++ b/solution.py
@@ -33,31 +33,58 @@
     return lax.broadcasted_iota(jnp.int32, shape, axis)
 
 
-def offset_peers(ep_size, me, step):
+def send_order(ep_size):
     if ep_size != 64:
-        return lax.rem(me + step, ep_size), lax.rem(me + ep_size - step, ep_size)
-    dy, dx = lax.rem(step // 4, 4), lax.rem(step, 4)
-    dz = lax.rem(step // 16 + 8 - dy - dx, 4)
+        return [(step,) for step in range(1, ep_size)] + [(0,)]
+
+    def at(axis, value, rest):
+        return tuple(rest[:axis]) + (value,) + tuple(rest[axis:])
+
+    def both(offset):
+        return [offset, tuple(-v % 4 for v in offset)]
+
+    order = [o for signs in ((1, 1, 1), (1, 1, 3), (1, 3, 1), (3, 1, 1)) for o in both(signs)]
+    for axis in range(3):
+        for rest in ((1, 1), (1, 3)):
+            order += both(at(axis, 2, rest)) + both(at(axis, 0, rest))
+    for axis in range(3):
+        order += both(at(axis, 1, (2, 2))) + both(at(axis, 1, (0, 0)))
+    for axis in range(3):
+        order += [at(axis, 2, (0, 0)), at(axis, 0, (2, 2))]
+    order += [(2, 2, 2)]
+    order += both((2, 1, 0)) + both((0, 2, 1)) + both((1, 0, 2)) + both((2, 0, 1)) + both((1, 2, 0)) + both((0, 1, 2))
+    return order + [(0, 0, 0)]
+
+
+def peer(ep_size, me, offset, sign):
+    if ep_size != 64:
+        return lax.rem(me + ep_size + sign * offset[0], ep_size)
     z, y, x = me // 16, lax.rem(me // 4, 4), lax.rem(me, 4)
-    ahead = lax.rem(z + dz, 4) * 16 + lax.rem(y + dy, 4) * 4 + lax.rem(x + dx, 4)
-    behind = lax.rem(z + 4 - dz, 4) * 16 + lax.rem(y + 4 - dy, 4) * 4 + lax.rem(x + 4 - dx, 4)
-    return ahead, behind
-
-
-def offset_step(ep_size, me, device):
+    dz, dy, dx = ((sign * v) % 4 for v in offset)
+    return lax.rem(z + dz, 4) * 16 + lax.rem(y + dy, 4) * 4 + lax.rem(x + dx, 4)
+
+
+def order_place(ep_size, me, device):
+    order = send_order(ep_size)
     if ep_size != 64:
         delta = device - me
-        return jnp.where(delta < 0, delta + ep_size, delta)
-    z, y, x = me // 16, lax.rem(me // 4, 4), lax.rem(me, 4)
-    dz, dy, dx = ((device >> 4) - z) & 3, (((device >> 2) & 3) - y) & 3, ((device & 3) - x) & 3
-    return (((dz + dy + dx) & 3) << 4) + (dy << 2) + dx
-
-
-def encoder_kernel(ep_size, groups, block, chunk, len_ref, idx_ref, x_hbm, gain_ref, shift_ref, wq_hbm, wk_hbm, wv_hbm, wo_hbm, bq_ref, bv_ref, bo_ref, f1_hbm, fb1_ref, f2_hbm, fb2_ref, wr_hbm, e1_hbm, eb1_ref, e2_hbm, eb2_ref, out_ref,
-                   hid_ref, wq_ref, wk_ref, wv_ref, wo_ref, f1_ref, f2_ref, wr_ref, e1_ref, e2_ref, load_sem, x_sem,
+        delta = jnp.where(delta < 0, delta + ep_size, delta)
+        codes = [offset[0] for offset in order]
+    else:
+        z, y, x = me // 16, lax.rem(me // 4, 4), lax.rem(me, 4)
+        delta = ((((device >> 4) - z) & 3) << 4) + (((((device >> 2) & 3) - y) & 3) << 2) + (((device & 3) - x) & 3)
+        codes = [16 * dz + 4 * dy + dx for dz, dy, dx in order]
+    place = jnp.zeros_like(device)
+    for index, code in enumerate(codes):
+        place = jnp.where(delta == code, index, place)
+    return place
+
+
+def encoder_kernel(ep_size, groups, block, chunk, len_ref, idx_hbm, x_hbm, gain_hbm, shift_hbm, wq_hbm, wk_hbm, wv_hbm, wo_hbm, bq_hbm, bv_hbm, bo_hbm, f1_hbm, fb1_hbm, f2_hbm, fb2_hbm, wr_hbm, e1_hbm, eb1_hbm, e2_hbm, eb2_hbm, out_hbm,
+                   hid_ref, wq_ref, wk_ref, wv_ref, wo_ref, f1_ref, f2_ref, wr_ref, e1_ref, e2_ref, idx_ref, gain_ref, shift_ref, bq_ref, bv_ref, bo_ref, fb1_ref, fb2_ref, eb1_ref, eb2_ref, load_sem, x_sem,
                    q_ref, kx_ref, vx_ref, ctx_ref, s_even, s_odd, p_even, p_odd, head_ref, part_ref, recv_ref, part_send, part_recv,
                    norm_ref, logit_ref, dest_ref, meta_ref, disp_ref, mine_ref, other_ref, keep_ref, give_ref, take_ref, done_ref, ret_ref,
-                   ship_send, ship_recv, swap_send, swap_recv, give_send, give_recv, back_send, back_recv, acc_ref, near_ref, far_ref, half_send, half_recv):
+                   ship_send, ship_recv, swap_send, swap_recv, give_send, give_recv, back_send, back_recv, acc_ref, near_ref, keep_sem, half_send, half_recv):
     me, core = lax.axis_index('ep'), lax.axis_index('tp')
     tokens, d_model = hid_ref.shape
     steps = tokens // block
@@ -78,30 +105,45 @@
     def x_copy(step):
         return pltpu.make_async_copy(x_hbm.at[rows_of(step)], hid_ref.at[rows_of(step)], x_sem.at[step])
 
-    pairs = [(wq_hbm, wq_ref), (wk_hbm, wk_ref), (wv_hbm, wv_ref), (wo_hbm, wo_ref), (f1_hbm, f1_ref), (f2_hbm, f2_ref), (wr_hbm, wr_ref), (e1_hbm, e1_ref), (e2_hbm, e2_ref)]
-    loads = [pltpu.make_async_copy(src, dst, load_sem.at[index]) for index, (src, dst) in enumerate(pairs)]
-    load_q, load_k, load_v, load_o, load_f1, load_f2, load_r, load_e1, load_e2 = loads
-
-    def fetch_x(step, carry):
+    loads = {}
+
+    def load(name, src, dst):
+        loads[name] = pltpu.make_async_copy(src, dst, load_sem.at[len(loads)])
+        loads[name].start()
+
+    def loaded(*names):
+        for name in names:
+            loads[name].wait()
+
+    for step in range(steps):
         x_copy(step).start()
-        return carry
-
-    lax.fori_loop(0, steps, fetch_x, 0)
-    for load in loads:
-        load.start()
-
-    def greet(step, carry):
-        pl.semaphore_signal(barrier, inc=1, device_id={'ep': offset_peers(ep_size, me, step)[0]}, device_id_type=MESH)
-        return carry
-
-    lax.fori_loop(1, ep_size, greet, 0)
+    load('gain', gain_hbm, gain_ref)
+    load('shift', shift_hbm, shift_ref)
+    load('q0', wq_hbm.at[0], wq_ref.at[0])
+    load('k0', wk_hbm.at[0], wk_ref.at[0])
+    load('v0', wv_hbm.at[0], wv_ref.at[0])
+    load('bq', bq_hbm, bq_ref)
+    load('bv', bv_hbm, bv_ref)
+    order = send_order(ep_size)
+    last = ep_size - 1
+    for offset in order[:last]:
+        pl.semaphore_signal(barrier, inc=1, device_id={'ep': peer(ep_size, me, offset, 1)}, device_id_type=MESH)
     pl.semaphore_signal(barrier, inc=1, device_id={'tp': 1 - core}, device_id_type=MESH)
 
     def exchange(stage, step):
         return to_partner(part_ref.at[rows_of(step)], recv_ref.at[stage % 2, rows_of(step)], part_send.at[stage, step], part_recv.at[stage, step])
 
+    def two_by_two(await_step, act):
+        def body(pair, carry):
+            for step in (2 * pair, 2 * pair + 1):
+                await_step(step)
+            for step in (2 * pair, 2 * pair + 1):
+                act(step)
+            return carry
+
+        lax.fori_loop(0, steps // 2, body, 0)
+
     def absorb(stage, step, bias):
-        exchange(stage, step).wait()
         total = part_ref[rows_of(step)].astype(F32) + recv_ref[stage % 2, rows_of(step)].astype(F32)
         hidden = (hid_ref[rows_of(step)].astype(F32) + total + bias).astype(BF16)
         hid_ref[rows_of(step)] = hidden
@@ -121,7 +163,7 @@
 
     def project(layer, step, normed):
         rows = rows_of(step)
-        bias_q, bias_v = bq_ref[layer], bv_ref[layer]
+        bias_q, bias_v = (jnp.concatenate([ref[head, layer:layer + 1] for head in range(width // 64)], axis=1) for ref in (bq_ref, bv_ref))
         query = (dot_nt(normed, wq_ref[layer]) + bias_q).astype(BF16)
         q_ref[rows] = (query.astype(F32) * 0.125).astype(BF16)
         keys = dot_nt(normed, wk_ref[layer])
@@ -162,42 +204,50 @@
             exchange(stage, step).start()
             return carry
 
-        lax.fori_loop(0, steps, body, 0)
+        lax.fori_loop(0, steps, body, 0, unroll=2)
 
     def normed_hidden(hidden, norm):
         return layer_norm(hidden, gain_ref[norm:norm + 1], shift_ref[norm:norm + 1]).astype(BF16)
 
-    load_q.wait()
-    load_k.wait()
-    load_v.wait()
-
-    def first_project(step, carry):
+    loaded('gain', 'shift', 'bq', 'bv', 'q0', 'k0', 'v0')
+    load('o', wo_hbm, wo_ref)
+    load('bo', bo_hbm, bo_ref)
+    load('f1', f1_hbm, f1_ref)
+    load('fb1', fb1_hbm, fb1_ref)
+    load('f2', f2_hbm, f2_ref)
+    load('fb2', fb2_hbm, fb2_ref)
+    for step in range(steps):
         x_copy(step).wait()
+    for step in range(steps):
         project(0, step, normed_hidden(hid_ref[rows_of(step)], 0))
-        return carry
-
-    lax.fori_loop(0, steps, first_project, 0)
-    load_o.wait()
+    loaded('o', 'bo', 'f1', 'fb1', 'f2', 'fb2')
+    load('q1', wq_hbm.at[1], wq_ref.at[1])
+    load('k1', wk_hbm.at[1], wk_ref.at[1])
+    load('v1', wv_hbm.at[1], wv_ref.at[1])
+    load('idx', idx_hbm, idx_ref)
+    load('r', wr_hbm, wr_ref)
+    load('e1', e1_hbm, e1_ref)
+    load('eb1', eb1_hbm, eb1_ref)
+    load('e2', e2_hbm, e2_ref)
+    load('eb2', eb2_hbm, eb2_ref)
     pl.semaphore_wait(barrier, ep_size)
     attend(0, 0)
-    load_f1.wait()
-    load_f2.wait()
-
-    def feed(step, carry):
+
+    def feed(step):
         normed = normed_hidden(absorb(0, step, bo_ref[0:1]), 1)
-        inner = jnp.maximum(dot_nn(normed, f1_ref[...]) + fb1_ref[...], 0.0).astype(BF16)
+        inner = jnp.maximum(dot_nn(normed, f1_ref[...]) + fb1_ref[...].reshape(1, -1), 0.0).astype(BF16)
         part_ref[rows_of(step)] = dot_nn(inner, f2_ref[...]).astype(BF16)
         exchange(1, step).start()
-        return carry
-
-    lax.fori_loop(0, steps, feed, 0)
-
-    def second_project(step, carry):
-        project(1, step, normed_hidden(absorb(1, step, fb2_ref[...]), 2))
-        return carry
-
-    lax.fori_loop(0, steps, second_project, 0)
+
+    two_by_two(lambda step: exchange(0, step).wait(), feed)
+    loaded('q1', 'k1', 'v1')
+
+    def second_project(step):
+        project(1, step, normed_hidden(absorb(1, step, fb2_ref[...].reshape(1, -1)), 2))
+
+    two_by_two(lambda step: exchange(1, step).wait(), second_project)
     attend(1, 2)
+    loaded('idx', 'r')
 
     valid = iota((1, tokens), 1) < len_ref[0]
     first, second = idx_ref[0:1], idx_ref[1:2]
@@ -210,33 +260,26 @@
     slot_first = jnp.sum(rank_first * hot_first, axis=0, keepdims=True).astype(jnp.int32)
     slot_second = jnp.sum(rank_second * hot_second, axis=0, keepdims=True).astype(jnp.int32)
 
-    def place(choice, slot):
-        step = offset_step(ep_size, me, choice >> 1)
-        return jnp.where(valid & (slot < cap), ((step << 1) + (choice & 1)) * cap + slot, experts * cap)
-
-    dest_ref[0:1] = place(first, slot_first)
-    dest_ref[1:2] = place(second, slot_second)
-    load_r.wait()
+    choice, slot = idx_ref[...], jnp.concatenate([slot_first, slot_second], axis=0)
+    home = ((order_place(ep_size, me, choice >> 1) << 1) + (choice & 1)) * cap + slot
+    dest_ref[0:2] = jnp.where(valid & (slot < cap), home, experts * cap)
     router = wr_ref[...].astype(BF16)
 
-    def settle(step, carry):
+    def settle(step):
         normed = normed_hidden(absorb(2, step, bo_ref[1:2]), 3)
         norm_ref[rows_of(step)] = normed
         logit_ref[rows_of(step)] = dot_nn(normed, router)
-        return carry
-
-    lax.fori_loop(0, steps, settle, 0)
+
+    two_by_two(lambda step: exchange(2, step).wait(), settle)
 
     def slot_rows(step):
-        return pl.ds(pl.multiple_of(lax.rem(step, each) * cap, cap), cap)
+        return pl.ds(step % each * cap, cap)
 
     def ship(step):
-        ahead, _ = offset_peers(ep_size, me, step)
-        return pltpu.make_async_remote_copy(src_ref=disp_ref.at[step // each, lax.rem(step, each)], dst_ref=mine_ref.at[step // each, :, slot_rows(step)], send_sem=ship_send.at[step], recv_sem=ship_recv.at[step], device_id={'ep': ahead}, device_id_type=MESH)
+        return pltpu.make_async_remote_copy(src_ref=disp_ref.at[step // each, step % each], dst_ref=mine_ref.at[step // each, :, slot_rows(step)], send_sem=ship_send.at[step], recv_sem=ship_recv.at[step], device_id={'ep': peer(ep_size, me, order[step], 1)}, device_id_type=MESH)
 
     def ship_back(step):
-        _, behind = offset_peers(ep_size, me, step)
-        return pltpu.make_async_remote_copy(src_ref=done_ref.at[step // each, :, slot_rows(step)], dst_ref=ret_ref.at[step // each, lax.rem(step, each)], send_sem=back_send.at[step], recv_sem=back_recv.at[step], device_id={'ep': behind}, device_id_type=MESH)
+        return pltpu.make_async_remote_copy(src_ref=done_ref.at[step // each, :, slot_rows(step)], dst_ref=ret_ref.at[step // each, step % each], send_sem=back_send.at[step], recv_sem=back_recv.at[step], device_id={'ep': peer(ep_size, me, order[step], -1)}, device_id_type=MESH)
 
     def swap(group):
         return to_partner(mine_ref.at[group], other_ref.at[group], swap_send.at[group], swap_recv.at[group])
@@ -245,11 +288,11 @@
         return to_partner(give_ref.at[group], take_ref.at[group], give_send.at[group], give_recv.at[group])
 
     def each_step(group, act):
-        def body(step, carry):
-            act(step)
-            return carry
-
-        lax.fori_loop(jnp.where(group == 0, 1, group * each), (group + 1) * each, body, 0)
+        for index in range(groups):
+            @pl.when(group == index)
+            def _(index=index):
+                for step in range(index * each, min((index + 1) * each, last)):
+                    act(step)
 
     members = each * local_experts * cap
 
@@ -261,7 +304,7 @@
         return carry
 
     lax.fori_loop(0, groups, scatter, 0)
-    mine_ref[0, :, 0:cap] = disp_ref[0, 0]
+    mine_ref[groups - 1, :, slot_rows(last)] = disp_ref[groups - 1, each - 1]
 
     row_id = iota((128, tokens), 0)
     packed = jnp.where(row_id == 0, dest_ref[0:1], jnp.where(row_id == 1, dest_ref[1:2], jnp.where(row_id == 2, first, second)))
@@ -280,8 +323,7 @@
         return carry
 
     lax.fori_loop(0, steps, gate, 0)
-    load_e1.wait()
-    load_e2.wait()
+    loaded('e1', 'eb1', 'e2', 'eb2')
 
     def deliver(group):
         give(group).wait_recv()
@@ -309,10 +351,13 @@
 
     lax.fori_loop(0, groups, work, 0)
     deliver(groups - 1)
-    ret_ref[0, 0] = done_ref[0, :, 0:cap]
+    ret_ref[groups - 1, each - 1] = done_ref[groups - 1, :, slot_rows(last)]
 
     def halves(step):
-        return to_partner(near_ref.at[rows_of(step)], far_ref.at[rows_of(step)], half_send.at[step], half_recv.at[step])
+        return to_partner(near_ref.at[rows_of(step)], out_hbm.at[rows_of(step), near], half_send.at[step], half_recv.at[step])
+
+    def keep(step):
+        return pltpu.make_async_copy(near_ref.at[rows_of(step)], out_hbm.at[rows_of(step), near], keep_sem.at[step])
 
     def gather(group, carry):
         each_step(group, lambda step: ship_back(step).wait_recv())
@@ -332,7 +377,7 @@
             def _():
                 near_ref[rows] = result.astype(BF16)
                 halves(step).start()
-                out_ref[rows, near] = result.astype(BF16)
+                keep(step).start()
 
             return carry
 
@@ -343,17 +388,13 @@
 
     def finish(step, carry):
         halves(step).wait()
-        out_ref[rows_of(step), far] = far_ref[rows_of(step)]
+        keep(step).wait()
         return carry
 
     lax.fori_loop(0, steps, finish, 0)
-
-    def drain(step, carry):
+    for step in range(last):
         ship(step).wait_send()
         ship_back(step).wait_send()
-        return carry
-
-    lax.fori_loop(1, ep_size, drain, 0)
 
     def drain_pairs(group, carry):
         swap(group).wait_send()
@@ -375,7 +416,7 @@
         half = d_model // 2
         groups = 4 if ep_size >= 16 else 2
         each = ep_size // groups
-        block, chunk = min(256, tokens // 2), 32
+        block, chunk = min(256, tokens // 2), 16
         steps = tokens // block
         w_q, w_k, w_v = (jnp.transpose(w, (0, 2, 3, 1)).reshape(2, width, d_model) for w in (w_query, w_key, w_value))
         w_o = w_attn_out.reshape(2, width, d_model)
@@ -383,7 +424,6 @@
         vmem = lambda *shape: pltpu.VMEM(shape, BF16)
         vmem32 = lambda *shape: pltpu.VMEM(shape, F32)
         dma = lambda *shape: pltpu.SemaphoreType.DMA(shape)
-        whole = pl.BlockSpec(memory_space=pltpu.VMEM)
         far_away = pl.BlockSpec(memory_space=pl.ANY)
         rows = each * cap
         wide = vmem(groups, local_experts, rows, half)
@@ -391,16 +431,17 @@
         result = pl.pallas_call(
             functools.partial(encoder_kernel, ep_size, groups, block, chunk),
             out_shape=jax.ShapeDtypeStruct((tokens, d_model), BF16),
-            in_specs=[pl.BlockSpec(memory_space=pltpu.SMEM), whole, far_away, whole, whole, far_away, far_away, far_away, far_away, whole, whole, whole, far_away, whole, far_away, whole, far_away, far_away, whole, far_away, whole],
-            out_specs=whole,
+            in_specs=[pl.BlockSpec(memory_space=pltpu.SMEM)] + [far_away] * 20,
+            out_specs=far_away,
             scratch_shapes=[
-                vmem(tokens, d_model), vmem(2, width, d_model), vmem(2, width, d_model), vmem(2, width, d_model), vmem(2, width, d_model), vmem(*w_fc1.shape), vmem(*w_fc2.shape), vmem32(*w_router.shape), vmem(*w_exp_in.shape), vmem(*w_exp_out.shape), dma(9), dma(steps),
+                vmem(tokens, d_model), vmem(2, width, d_model), vmem(2, width, d_model), vmem(2, width, d_model), vmem(2, width, d_model), vmem(*w_fc1.shape), vmem(*w_fc2.shape), vmem32(*w_router.shape), vmem(*w_exp_in.shape), vmem(*w_exp_out.shape),
+                pltpu.VMEM((2, tokens), jnp.int32), vmem32(4, d_model), vmem32(4, d_model), vmem32(width // 64, 2, 64), vmem32(width // 64, 2, 64), vmem32(2, d_model), vmem32(*b_fc1.shape), vmem32(*b_fc2.shape), vmem32(*b_exp_in.shape), vmem32(*b_exp_out.shape), dma(24), dma(steps),
                 vmem(tokens, width), vmem(width // 64, tokens, 128), vmem(width // 64, tokens, 128), vmem(block, width), vmem32(block, tokens), vmem32(block, tokens), vmem(block, tokens), vmem(block, tokens), vmem32(block, 128), vmem(tokens, d_model), vmem(2, tokens, d_model), dma(3, steps), dma(3, steps),
                 vmem(tokens, d_model), vmem32(tokens, num_experts), pltpu.VMEM((8, tokens), jnp.int32), vmem32(tokens, 128), blocks, wide, wide, vmem(local_experts, rows, half), wide, wide, wide, blocks,
-                dma(ep_size), dma(ep_size), dma(groups), dma(groups), dma(groups), dma(groups), dma(ep_size), dma(ep_size), vmem32(tokens, half), vmem(tokens, half), vmem(tokens, half), dma(steps), dma(steps),
+                dma(ep_size), dma(ep_size), dma(groups), dma(groups), dma(groups), dma(groups), dma(ep_size), dma(ep_size), vmem32(tokens, half), vmem(tokens, half), dma(steps), dma(steps), dma(steps),
             ],
             compiler_params=pltpu.CompilerParams(collective_id=1, has_side_effects=True, vmem_limit_bytes=67043328),
-        )(src_len, idx, x.reshape(tokens, d_model), ln_gain, ln_bias, w_q, w_k, w_v, w_o, b_query.reshape(2, 1, width), b_value.reshape(2, 1, width), b_attn_out, w_fc1, b_fc1.reshape(1, -1), w_fc2, b_fc2.reshape(1, -1), w_router, w_exp_in, b_exp_in, w_exp_out, b_exp_out)
+        )(src_len, idx, x.reshape(tokens, d_model), ln_gain, ln_bias, w_q, w_k, w_v, w_o, jnp.transpose(b_query, (1, 0, 2)), jnp.transpose(b_value, (1, 0, 2)), b_attn_out, w_fc1, b_fc1, w_fc2, b_fc2, w_router, w_exp_in, b_exp_in, w_exp_out, b_exp_out)
         return result.reshape(1, tokens, d_model)
 
     in_specs = (P(('dp', 'ep'), None, None), P(('dp', 'ep')), P(('dp', 'ep'), None, None), P(), P(), P(None, None, 'tp', None), P(None, 'tp', None), P(None, None, 'tp', None), P(None, None, 'tp', None), P(None, 'tp', None), P(None, 'tp', None, None), P(), P(None, 'tp'), P('tp'), P('tp', None), P(), P(), P('ep', None, 'tp'), P('ep', 'tp'), P('ep', 'tp', None), P('ep', None))

time: 116 us -> 110 us (0.948); the launches traced: 116 us -> 108 us
  local copies, waits for them, and re-layouts: 7.91 us -> 2.65 us
  Pallas kernels: 108 us -> 105 us
    reshape x4 -> x0, local copies, waits for them, and re-layouts: 3.87 us -> none  [the longest x1 1.29 us: local_fn(): b_fc1.reshape(1, -1)]
    pallas_call x1, Pallas kernels: 108 us -> 105 us  [local_fn(): pl.pallas_call(functools.partial(encoder_kernel, ep_size, groups, block,...]
    unnamed x3 -> x1, local copies, waits for them, and re-layouts: 4.04 us -> 2.65 us
where the time goes in v1:
time: 110 us; the launch traced here: 108 us
  Pallas kernels  105 us (95%)
  local copies, waits for them, and re-layouts  2.65 us (2%)
    pallas_call x1, Pallas kernels, local_fn(): pl.pallas_call(functools.partial(encoder_kernel, ep_size, groups, block,...  105 us
    unnamed x1, local copies, waits for them, and re-layouts  2.65 us

profile of v1, /device:TPU:1, one launch (start us, length us, event | category | flops | bytes accessed | tf_op | source)
XLA Modules:
  0.0 107.9 jit_solution(6325826758907901948)
XLA Ops:
  0.7 104.6 %shard_map.199 = bf16[1024,768]{1,0:T(8,128)(2,1)} custom-call(s32[1]{0:T(128)S(6)} %copy.23.len_ref, s32[2,1024]{1,0:T(2,128)} %bitcast.23, bf16[1024,768]{1,0:T(8,128)(2,1)} %bitcast.18, f32[4,768]{1,0:T(4,128)} %gain_hbm.1, f32[4,768]{1,0:T(4,128)} %shift_hbm.1, bf16[2,384,768]{2,1,0:T(8,128)(2,1)} %bitcast.19, bf16[2,384,768]{2,1,0:T(8,128)(2,1)} %bitcast.20, ...), custom_call_target="tpu_custom_call" | custom-call | tf_op jit(solution)/shard_map/pallas_call | solution.py:431
  105.3 2.7 %copy.24 = bf16[1,1024,768]{2,1,0:T(8,128)(2,1)} copy(bf16[1,1024,768]{2,1,0:T(8,128)(2,1)} %bitcast.17) | data formatting | bytes 3145728

commit v2 on v1

--- a/solution.py
+++ b/solution.py
@@ -84,7 +84,7 @@
                    hid_ref, wq_ref, wk_ref, wv_ref, wo_ref, f1_ref, f2_ref, wr_ref, e1_ref, e2_ref, idx_ref, gain_ref, shift_ref, bq_ref, bv_ref, bo_ref, fb1_ref, fb2_ref, eb1_ref, eb2_ref, load_sem, x_sem,
                    q_ref, kx_ref, vx_ref, ctx_ref, s_even, s_odd, p_even, p_odd, head_ref, part_ref, recv_ref, part_send, part_recv,
                    norm_ref, logit_ref, dest_ref, meta_ref, disp_ref, mine_ref, other_ref, keep_ref, give_ref, take_ref, done_ref, ret_ref,
-                   ship_send, ship_recv, swap_send, swap_recv, give_send, give_recv, back_send, back_recv, acc_ref, near_ref, keep_sem, half_send, half_recv):
+                   ship_send, ship_recv, swap_send, swap_recv, give_send, give_recv, back_send, back_recv, acc_ref, near_ref, keep_sem, half_send, half_recv, hot_ref):
     me, core = lax.axis_index('ep'), lax.axis_index('tp')
     tokens, d_model = hid_ref.shape
     steps = tokens // block
@@ -149,7 +149,11 @@
         hid_ref[rows_of(step)] = hidden
         return hidden
 
-    lane = iota((block, 128), 1)
+    lane = iota((2 * block, 128), 1)
+
+    def rows_of_pair(pair):
+        return pl.ds(pl.multiple_of(2 * pair * block, 2 * block), 2 * block)
+
     key_ok = iota((chunk, tokens - MIN_LEN), 1) + MIN_LEN < len_ref[0] if tokens > MIN_LEN else None
 
     def softmax(s_ref, p_ref):
@@ -161,8 +165,8 @@
             scale = 1.0 / jnp.sum(weights, axis=-1, keepdims=True)
             p_ref[start:start + chunk] = (weights * scale).astype(BF16)
 
-    def project(layer, step, normed):
-        rows = rows_of(step)
+    def project(layer, pair, normed):
+        rows = rows_of_pair(pair)
         bias_q, bias_v = (jnp.concatenate([ref[head, layer:layer + 1] for head in range(width // 64)], axis=1) for ref in (bq_ref, bv_ref))
         query = (dot_nt(normed, wq_ref[layer]) + bias_q).astype(BF16)
         q_ref[rows] = (query.astype(F32) * 0.125).astype(BF16)
@@ -218,8 +222,8 @@
     load('fb2', fb2_hbm, fb2_ref)
     for step in range(steps):
         x_copy(step).wait()
-    for step in range(steps):
-        project(0, step, normed_hidden(hid_ref[rows_of(step)], 0))
+    for pair in range(steps // 2):
+        project(0, pair, normed_hidden(hid_ref[rows_of_pair(pair)], 0))
     loaded('o', 'bo', 'f1', 'fb1', 'f2', 'fb2')
     load('q1', wq_hbm.at[1], wq_ref.at[1])
     load('k1', wk_hbm.at[1], wk_ref.at[1])
@@ -233,19 +237,27 @@
     pl.semaphore_wait(barrier, ep_size)
     attend(0, 0)
 
-    def feed(step):
-        normed = normed_hidden(absorb(0, step, bo_ref[0:1]), 1)
+    def feed(pair, carry):
+        for step in (2 * pair, 2 * pair + 1):
+            exchange(0, step).wait()
+        normed = jnp.concatenate([normed_hidden(absorb(0, step, bo_ref[0:1]), 1) for step in (2 * pair, 2 * pair + 1)], axis=0)
         inner = jnp.maximum(dot_nn(normed, f1_ref[...]) + fb1_ref[...].reshape(1, -1), 0.0).astype(BF16)
-        part_ref[rows_of(step)] = dot_nn(inner, f2_ref[...]).astype(BF16)
-        exchange(1, step).start()
-
-    two_by_two(lambda step: exchange(0, step).wait(), feed)
+        part_ref[rows_of_pair(pair)] = dot_nn(inner, f2_ref[...]).astype(BF16)
+        for step in (2 * pair, 2 * pair + 1):
+            exchange(1, step).start()
+        return carry
+
+    lax.fori_loop(0, steps // 2, feed, 0)
     loaded('q1', 'k1', 'v1')
 
-    def second_project(step):
-        project(1, step, normed_hidden(absorb(1, step, fb2_ref[...].reshape(1, -1)), 2))
-
-    two_by_two(lambda step: exchange(1, step).wait(), second_project)
+    def second_project(pair, carry):
+        both = (2 * pair, 2 * pair + 1)
+        for step in both:
+            exchange(1, step).wait()
+        project(1, pair, jnp.concatenate([normed_hidden(absorb(1, step, fb2_ref[...].reshape(1, -1)), 2) for step in both], axis=0))
+        return carry
+
+    lax.fori_loop(0, steps // 2, second_project, 0)
     attend(1, 2)
     loaded('idx', 'r')
 
@@ -284,8 +296,8 @@
     def swap(group):
         return to_partner(mine_ref.at[group], other_ref.at[group], swap_send.at[group], swap_recv.at[group])
 
-    def give(group):
-        return to_partner(give_ref.at[group], take_ref.at[group], give_send.at[group], give_recv.at[group])
+    def give(group, expert):
+        return to_partner(give_ref.at[group, expert], take_ref.at[group, expert], give_send.at[group, expert], give_recv.at[group, expert])
 
     def each_step(group, act):
         for index in range(groups):
@@ -311,6 +323,7 @@
     meta_ref[...] = packed.astype(F32).T
     column = iota((block, experts), 1).astype(F32)
     spot = iota((block, 128), 1)
+    slots = iota((block, members), 1)
 
     def gate(step, carry):
         table, logits = meta_ref[rows_of(step)], logit_ref[rows_of(step)]
@@ -320,37 +333,49 @@
         gate_second = jax.nn.sigmoid(logit_second - logit_first)
         meta_ref[rows_of(step)] = jnp.where(spot == 2, gate_first, jnp.where(spot == 3, gate_second, table))
         acc_ref[rows_of(step)] = hid_ref[rows_of(step), near].astype(F32)
+        dest = table.astype(jnp.int32)
+        for group in range(groups):
+            for choice in range(2):
+                hot_ref[group, step, choice * block:(choice + 1) * block] = jnp.where(slots == dest[:, choice:choice + 1] - group * members, 1.0, 0.0).astype(BF16)
         return carry
 
     lax.fori_loop(0, steps, gate, 0)
     loaded('e1', 'eb1', 'e2', 'eb2')
 
     def deliver(group):
-        give(group).wait_recv()
         for expert in range(local_experts):
+            give(group, expert).wait_recv()
             total = keep_ref[expert].astype(F32) + take_ref[group, expert].astype(F32)
             done_ref[group, expert] = (total + eb2_ref[expert:expert + 1, near]).astype(BF16)
         each_step(group, lambda step: ship_back(step).start())
 
-    def work(group, carry):
+    def arrive(group):
         each_step(group, lambda step: ship(step).wait_recv())
         swap(group).start()
 
-        @pl.when(group > 0)
-        def _():
-            deliver(group - 1)
-
+    def work(group, carry):
         swap(group).wait_recv()
         for expert in range(local_experts):
             inner = dot_nn(mine_ref[group, expert], e1_ref[expert, near]) + dot_nn(other_ref[group, expert], e1_ref[expert, far])
             inner = jnp.maximum(inner + eb1_ref[expert:expert + 1], 0.0).astype(BF16)
             give_ref[group, expert] = dot_nn(inner, e2_ref[expert, :, far]).astype(BF16)
+            give(group, expert).start()
             keep_ref[expert] = dot_nn(inner, e2_ref[expert, :, near]).astype(BF16)
-        give(group).start()
-        return carry
-
+            if expert == 0:
+                @pl.when((group > 0) & (group < groups - 1))
+                def _():
+                    arrive(group + 1)
+
+        deliver(group)
+
+        @pl.when(group == 0)
+        def _():
+            arrive(1)
+
+        return carry
+
+    arrive(0)
     lax.fori_loop(0, groups, work, 0)
-    deliver(groups - 1)
     ret_ref[groups - 1, each - 1] = done_ref[groups - 1, :, slot_rows(last)]
 
     def halves(step):
@@ -359,32 +384,32 @@
     def keep(step):
         return pltpu.make_async_copy(near_ref.at[rows_of(step)], out_hbm.at[rows_of(step), near], keep_sem.at[step])
 
+    def pick(group, step):
+        rows = rows_of(step)
+        table = meta_ref[rows]
+        picked = dot_nn(hot_ref[group, step], ret_ref[group].reshape(members, half))
+        return acc_ref[rows] + (table[:, 2:3] * picked[:block] + table[:, 3:4] * picked[block:])
+
     def gather(group, carry):
         each_step(group, lambda step: ship_back(step).wait_recv())
-        slots = iota((block, members), 1) + group * members
-
-        def pick(step, carry):
-            rows = rows_of(step)
-            table = meta_ref[rows]
-            dest = table.astype(jnp.int32)
-            returned = ret_ref[group].reshape(members, half)
-            one = dot_nn(jnp.where(slots == dest[:, 0:1], 1.0, 0.0).astype(BF16), returned)
-            two = dot_nn(jnp.where(slots == dest[:, 1:2], 1.0, 0.0).astype(BF16), returned)
-            result = acc_ref[rows] + (table[:, 2:3] * one + table[:, 3:4] * two)
-            acc_ref[rows] = result
-
-            @pl.when(group == groups - 1)
-            def _():
-                near_ref[rows] = result.astype(BF16)
-                halves(step).start()
-                keep(step).start()
-
+
+        def body(step, carry):
+            acc_ref[rows_of(step)] = pick(group, step)
             return carry
 
-        lax.fori_loop(0, steps, pick, 0)
-        return carry
-
-    lax.fori_loop(0, groups, gather, 0)
+        lax.fori_loop(0, steps, body, 0, unroll=True)
+        return carry
+
+    lax.fori_loop(0, groups - 1, gather, 0)
+    each_step(groups - 1, lambda step: ship_back(step).wait_recv())
+
+    def complete(step, carry):
+        near_ref[rows_of(step)] = pick(groups - 1, step).astype(BF16)
+        halves(step).start()
+        keep(step).start()
+        return carry
+
+    lax.fori_loop(0, steps, complete, 0, unroll=True)
 
     def finish(step, carry):
         halves(step).wait()
@@ -398,7 +423,8 @@
 
     def drain_pairs(group, carry):
         swap(group).wait_send()
-        give(group).wait_send()
+        for expert in range(local_experts):
+            give(group, expert).wait_send()
         return carry
 
     lax.fori_loop(0, groups, drain_pairs, 0)
@@ -438,7 +464,7 @@
                 pltpu.VMEM((2, tokens), jnp.int32), vmem32(4, d_model), vmem32(4, d_model), vmem32(width // 64, 2, 64), vmem32(width // 64, 2, 64), vmem32(2, d_model), vmem32(*b_fc1.shape), vmem32(*b_fc2.shape), vmem32(*b_exp_in.shape), vmem32(*b_exp_out.shape), dma(24), dma(steps),
                 vmem(tokens, width), vmem(width // 64, tokens, 128), vmem(width // 64, tokens, 128), vmem(block, width), vmem32(block, tokens), vmem32(block, tokens), vmem(block, tokens), vmem(block, tokens), vmem32(block, 128), vmem(tokens, d_model), vmem(2, tokens, d_model), dma(3, steps), dma(3, steps),
                 vmem(tokens, d_model), vmem32(tokens, num_experts), pltpu.VMEM((8, tokens), jnp.int32), vmem32(tokens, 128), blocks, wide, wide, vmem(local_experts, rows, half), wide, wide, wide, blocks,
-                dma(ep_size), dma(ep_size), dma(groups), dma(groups), dma(groups), dma(groups), dma(ep_size), dma(ep_size), vmem32(tokens, half), vmem(tokens, half), dma(steps), dma(steps), dma(steps),
+                dma(ep_size), dma(ep_size), dma(groups), dma(groups), dma(groups, local_experts), dma(groups, local_experts), dma(ep_size), dma(ep_size), vmem32(tokens, half), vmem(tokens, half), dma(steps), dma(steps), dma(steps), vmem(groups, steps, 2 * block, each * local_experts * cap),
             ],
             compiler_params=pltpu.CompilerParams(collective_id=1, has_side_effects=True, vmem_limit_bytes=67043328),
         )(src_len, idx, x.reshape(tokens, d_model), ln_gain, ln_bias, w_q, w_k, w_v, w_o, jnp.transpose(b_query, (1, 0, 2)), jnp.transpose(b_value, (1, 0, 2)), b_attn_out, w_fc1, b_fc1, w_fc2, b_fc2, w_router, w_exp_in, b_exp_in, w_exp_out, b_exp_out)

time: 110 us -> 107 us (0.973)
  Pallas kernels: 105 us -> 101 us
    pallas_call x1, Pallas kernels: 105 us -> 101 us  [local_fn(): pl.pallas_call(functools.partial(encoder_kernel, ep_size, groups, block,...]
where the time goes in v2:
time: 107 us; the launch traced here: 105 us
  Pallas kernels  101 us (94%)
  local copies, waits for them, and re-layouts  2.65 us (2%)
    pallas_call x1, Pallas kernels, local_fn(): pl.pallas_call(functools.partial(encoder_kernel, ep_size, groups, block,...  101 us
    unnamed x1, local copies, waits for them, and re-layouts  2.65 us

profile of v2, /device:TPU:1, one launch (start us, length us, event | category | flops | bytes accessed | tf_op | source)
XLA Modules:
  0.0 104.7 jit_solution(1494755323182370986)
XLA Ops:
  0.7 101.4 %shard_map.199 = bf16[1024,768]{1,0:T(8,128)(2,1)} custom-call(s32[1]{0:T(128)S(6)} %copy.23.len_ref, s32[2,1024]{1,0:T(2,128)} %bitcast.23, bf16[1024,768]{1,0:T(8,128)(2,1)} %bitcast.18, f32[4,768]{1,0:T(4,128)} %gain_hbm.1, f32[4,768]{1,0:T(4,128)} %shift_hbm.1, bf16[2,384,768]{2,1,0:T(8,128)(2,1)} %bitcast.19, bf16[2,384,768]{2,1,0:T(8,128)(2,1)} %bitcast.20, ...), custom_call_target="tpu_custom_call" | custom-call | tf_op jit(solution)/shard_map/pallas_call | solution.py:457
  102.1 2.7 %copy.24 = bf16[1,1024,768]{2,1,0:T(8,128)(2,1)} copy(bf16[1,1024,768]{2,1,0:T(8,128)(2,1)} %bitcast.17) | data formatting | bytes 3145728

commit v3 on v2

--- a/solution.py
+++ b/solution.py
@@ -299,8 +299,8 @@
     def give(group, expert):
         return to_partner(give_ref.at[group, expert], take_ref.at[group, expert], give_send.at[group, expert], give_recv.at[group, expert])
 
-    def each_step(group, act):
-        for index in range(groups):
+    def each_step(group, act, among=range(groups)):
+        for index in among:
             @pl.when(group == index)
             def _(index=index):
                 for step in range(index * each, min((index + 1) * each, last)):
@@ -312,7 +312,7 @@
         slots = iota((members, tokens), 0) + group * members
         taken = jnp.where((slots == dest_ref[0:1]) | (slots == dest_ref[1:2]), 1.0, 0.0).astype(BF16)
         disp_ref[group] = dot_nn(taken, norm_ref[:, near]).astype(BF16).reshape(each, local_experts, cap, half)
-        each_step(group, lambda step: ship(step).start())
+        each_step(group, lambda step: ship(step).start(), range(groups - 1))
         return carry
 
     lax.fori_loop(0, groups, scatter, 0)
@@ -355,6 +355,12 @@
 
     def work(group, carry):
         swap(group).wait_recv()
+
+        @pl.when(group == 0)
+        def _():
+            for step in range((groups - 1) * each, last):
+                ship(step).start()
+
         for expert in range(local_experts):
             inner = dot_nn(mine_ref[group, expert], e1_ref[expert, near]) + dot_nn(other_ref[group, expert], e1_ref[expert, far])
             inner = jnp.maximum(inner + eb1_ref[expert:expert + 1], 0.0).astype(BF16)
@@ -409,7 +415,7 @@
         keep(step).start()
         return carry
 
-    lax.fori_loop(0, steps, complete, 0, unroll=True)
+    lax.fori_loop(0, steps, complete, 0, unroll=2)
 
     def finish(step, carry):
         halves(step).wait()

time: 107 us -> 109 us (1.019); the launches traced: 105 us -> 108 us
  Pallas kernels: 101 us -> 105 us
    pallas_call x1, Pallas kernels: 101 us -> 105 us  [local_fn(): pl.pallas_call(functools.partial(encoder_kernel, ep_size, groups, block,...]
where the time goes in v3:
time: 109 us; the launch traced here: 108 us
  Pallas kernels  105 us (96%)
  local copies, waits for them, and re-layouts  2.65 us (2%)
    pallas_call x1, Pallas kernels, local_fn(): pl.pallas_call(functools.partial(encoder_kernel, ep_size, groups, block,...  105 us
    unnamed x1, local copies, waits for them, and re-layouts  2.65 us

profile of v3, /device:TPU:1, one launch (start us, length us, event | category | flops | bytes accessed | tf_op | source)
XLA Modules:
  0.0 107.9 jit_solution(8828708961080800859)
XLA Ops:
  0.7 104.6 %shard_map.199 = bf16[1024,768]{1,0:T(8,128)(2,1)} custom-call(s32[1]{0:T(128)S(6)} %copy.23.len_ref, s32[2,1024]{1,0:T(2,128)} %bitcast.23, bf16[1024,768]{1,0:T(8,128)(2,1)} %bitcast.18, f32[4,768]{1,0:T(4,128)} %gain_hbm.1, f32[4,768]{1,0:T(4,128)} %shift_hbm.1, bf16[2,384,768]{2,1,0:T(8,128)(2,1)} %bitcast.19, bf16[2,384,768]{2,1,0:T(8,128)(2,1)} %bitcast.20, ...), custom_call_target="tpu_custom_call" | custom-call | tf_op jit(solution)/shard_map/pallas_call | solution.py:463
  105.3 2.7 %copy.24 = bf16[1,1024,768]{2,1,0:T(8,128)(2,1)} copy(bf16[1,1024,768]{2,1,0:T(8,128)(2,1)} %bitcast.17) | data formatting | bytes 3145728

commit v4 on v2

--- a/solution.py
+++ b/solution.py
@@ -83,7 +83,7 @@
 def encoder_kernel(ep_size, groups, block, chunk, len_ref, idx_hbm, x_hbm, gain_hbm, shift_hbm, wq_hbm, wk_hbm, wv_hbm, wo_hbm, bq_hbm, bv_hbm, bo_hbm, f1_hbm, fb1_hbm, f2_hbm, fb2_hbm, wr_hbm, e1_hbm, eb1_hbm, e2_hbm, eb2_hbm, out_hbm,
                    hid_ref, wq_ref, wk_ref, wv_ref, wo_ref, f1_ref, f2_ref, wr_ref, e1_ref, e2_ref, idx_ref, gain_ref, shift_ref, bq_ref, bv_ref, bo_ref, fb1_ref, fb2_ref, eb1_ref, eb2_ref, load_sem, x_sem,
                    q_ref, kx_ref, vx_ref, ctx_ref, s_even, s_odd, p_even, p_odd, head_ref, part_ref, recv_ref, part_send, part_recv,
-                   norm_ref, logit_ref, dest_ref, meta_ref, disp_ref, mine_ref, other_ref, keep_ref, give_ref, take_ref, done_ref, ret_ref,
+                   norm_ref, logit_ref, dest_ref, meta_ref, disp_ref, joint_ref, sum_ref, take_ref, done_ref, ret_ref,
                    ship_send, ship_recv, swap_send, swap_recv, give_send, give_recv, back_send, back_recv, acc_ref, near_ref, keep_sem, half_send, half_recv, hot_ref):
     me, core = lax.axis_index('ep'), lax.axis_index('tp')
     tokens, d_model = hid_ref.shape
@@ -288,16 +288,16 @@
         return pl.ds(step % each * cap, cap)
 
     def ship(step):
-        return pltpu.make_async_remote_copy(src_ref=disp_ref.at[step // each, step % each], dst_ref=mine_ref.at[step // each, :, slot_rows(step)], send_sem=ship_send.at[step], recv_sem=ship_recv.at[step], device_id={'ep': peer(ep_size, me, order[step], 1)}, device_id_type=MESH)
+        return pltpu.make_async_remote_copy(src_ref=disp_ref.at[step // each, step % each], dst_ref=joint_ref.at[step // each, :, slot_rows(step), near], send_sem=ship_send.at[step], recv_sem=ship_recv.at[step], device_id={'ep': peer(ep_size, me, order[step], 1)}, device_id_type=MESH)
 
     def ship_back(step):
         return pltpu.make_async_remote_copy(src_ref=done_ref.at[step // each, :, slot_rows(step)], dst_ref=ret_ref.at[step // each, step % each], send_sem=back_send.at[step], recv_sem=back_recv.at[step], device_id={'ep': peer(ep_size, me, order[step], -1)}, device_id_type=MESH)
 
     def swap(group):
-        return to_partner(mine_ref.at[group], other_ref.at[group], swap_send.at[group], swap_recv.at[group])
+        return to_partner(joint_ref.at[group, :, :, near], joint_ref.at[group, :, :, near], swap_send.at[group], swap_recv.at[group])
 
     def give(group, expert):
-        return to_partner(give_ref.at[group, expert], take_ref.at[group, expert], give_send.at[group, expert], give_recv.at[group, expert])
+        return to_partner(sum_ref.at[group, expert, :, far], take_ref.at[group, expert], give_send.at[group, expert], give_recv.at[group, expert])
 
     def each_step(group, act):
         for index in range(groups):
@@ -316,7 +316,7 @@
         return carry
 
     lax.fori_loop(0, groups, scatter, 0)
-    mine_ref[groups - 1, :, slot_rows(last)] = disp_ref[groups - 1, each - 1]
+    joint_ref[groups - 1, :, slot_rows(last), near] = disp_ref[groups - 1, each - 1]
 
     row_id = iota((128, tokens), 0)
     packed = jnp.where(row_id == 0, dest_ref[0:1], jnp.where(row_id == 1, dest_ref[1:2], jnp.where(row_id == 2, first, second)))
@@ -345,7 +345,7 @@
     def deliver(group):
         for expert in range(local_experts):
             give(group, expert).wait_recv()
-            total = keep_ref[expert].astype(F32) + take_ref[group, expert].astype(F32)
+            total = sum_ref[group, expert, :, near].astype(F32) + take_ref[group, expert].astype(F32)
             done_ref[group, expert] = (total + eb2_ref[expert:expert + 1, near]).astype(BF16)
         each_step(group, lambda step: ship_back(step).start())
 
@@ -356,11 +356,9 @@
     def work(group, carry):
         swap(group).wait_recv()
         for expert in range(local_experts):
-            inner = dot_nn(mine_ref[group, expert], e1_ref[expert, near]) + dot_nn(other_ref[group, expert], e1_ref[expert, far])
-            inner = jnp.maximum(inner + eb1_ref[expert:expert + 1], 0.0).astype(BF16)
-            give_ref[group, expert] = dot_nn(inner, e2_ref[expert, :, far]).astype(BF16)
+            inner = jnp.maximum(dot_nn(joint_ref[group, expert], e1_ref[expert]) + eb1_ref[expert:expert + 1], 0.0).astype(BF16)
+            sum_ref[group, expert] = dot_nn(inner, e2_ref[expert]).astype(BF16)
             give(group, expert).start()
-            keep_ref[expert] = dot_nn(inner, e2_ref[expert, :, near]).astype(BF16)
             if expert == 0:
                 @pl.when((group > 0) & (group < groups - 1))
                 def _():
@@ -453,6 +451,7 @@
         far_away = pl.BlockSpec(memory_space=pl.ANY)
         rows = each * cap
         wide = vmem(groups, local_experts, rows, half)
+        full = vmem(groups, local_experts, rows, d_model)
         blocks = vmem(groups, each, local_experts, cap, half)
         result = pl.pallas_call(
             functools.partial(encoder_kernel, ep_size, groups, block, chunk),
@@ -463,7 +462,7 @@
                 vmem(tokens, d_model), vmem(2, width, d_model), vmem(2, width, d_model), vmem(2, width, d_model), vmem(2, width, d_model), vmem(*w_fc1.shape), vmem(*w_fc2.shape), vmem32(*w_router.shape), vmem(*w_exp_in.shape), vmem(*w_exp_out.shape),
                 pltpu.VMEM((2, tokens), jnp.int32), vmem32(4, d_model), vmem32(4, d_model), vmem32(width // 64, 2, 64), vmem32(width // 64, 2, 64), vmem32(2, d_model), vmem32(*b_fc1.shape), vmem32(*b_fc2.shape), vmem32(*b_exp_in.shape), vmem32(*b_exp_out.shape), dma(24), dma(steps),
                 vmem(tokens, width), vmem(width // 64, tokens, 128), vmem(width // 64, tokens, 128), vmem(block, width), vmem32(block, tokens), vmem32(block, tokens), vmem(block, tokens), vmem(block, tokens), vmem32(block, 128), vmem(tokens, d_model), vmem(2, tokens, d_model), dma(3, steps), dma(3, steps),
-                vmem(tokens, d_model), vmem32(tokens, num_experts), pltpu.VMEM((8, tokens), jnp.int32), vmem32(tokens, 128), blocks, wide, wide, vmem(local_experts, rows, half), wide, wide, wide, blocks,
+                vmem(tokens, d_model), vmem32(tokens, num_experts), pltpu.VMEM((8, tokens), jnp.int32), vmem32(tokens, 128), blocks, full, full, wide, wide, blocks,
                 dma(ep_size), dma(ep_size), dma(groups), dma(groups), dma(groups, local_experts), dma(groups, local_experts), dma(ep_size), dma(ep_size), vmem32(tokens, half), vmem(tokens, half), dma(steps), dma(steps), dma(steps), vmem(groups, steps, 2 * block, each * local_experts * cap),
             ],
             compiler_params=pltpu.CompilerParams(collective_id=1, has_side_effects=True, vmem_limit_bytes=67043328),

time: 107 us -> 105 us (0.981); the launches traced: 105 us -> 104 us
  no operation moved by 1% of the time
where the time goes in v4:
time: 105 us; the launch traced here: 104 us
  Pallas kernels  101 us (96%)
  local copies, waits for them, and re-layouts  2.65 us (3%)
    pallas_call x1, Pallas kernels, local_fn(): pl.pallas_call(functools.partial(encoder_kernel, ep_size, groups, block,...  101 us
    unnamed x1, local copies, waits for them, and re-layouts  2.65 us

profile of v4, /device:TPU:1, one launch (start us, length us, event | category | flops | bytes accessed | tf_op | source)
XLA Modules:
  0.0 104.4 jit_solution(10908692263329033402)
XLA Ops:
  0.7 101.0 %shard_map.199 = bf16[1024,768]{1,0:T(8,128)(2,1)} custom-call(s32[1]{0:T(128)S(6)} %copy.23.len_ref, s32[2,1024]{1,0:T(2,128)} %bitcast.23, bf16[1024,768]{1,0:T(8,128)(2,1)} %bitcast.18, f32[4,768]{1,0:T(4,128)} %gain_hbm.1, f32[4,768]{1,0:T(4,128)} %shift_hbm.1, bf16[2,384,768]{2,1,0:T(8,128)(2,1)} %bitcast.19, bf16[2,384,768]{2,1,0:T(8,128)(2,1)} %bitcast.20, ...), custom_call_target="tpu_custom_call" | custom-call | tf_op jit(solution)/shard_map/pallas_call | solution.py:456
  101.7 2.7 %copy.24 = bf16[1,1024,768]{2,1,0:T(8,128)(2,1)} copy(bf16[1,1024,768]{2,1,0:T(8,128)(2,1)} %bitcast.17) | data formatting | bytes 3145728
